TPU v7x, 512 devices: a 8x2x16 block of a 8x8x16 slice. The times are simulated.
512 devices in a mesh: cfg: 2 (over y), gx: 128 (over x, z), gy: 2 (over core).
Axes of the slice: x: 8, y: 2, z: 16, core: 2. Of those that a mesh axis runs over, the one named last changes fastest.
The devices are a block of a 8x8x16 slice.
Arguments:
- gauge_links: float32 [4, 12, 256, 16, 1024], P(None, None, ('cfg', 'gx'), 'gy'), parts along dimension 2, may hold values from -1 to 1, as said below
- momentum: float32 [8, 256, 16, 1024], P(None, ('cfg', 'gx'), 'gy'), parts along dimension 1, may hold values from -6 to 6
Outputs:
- new_momentum: float32 [8, 256, 16, 1024], P(None, ('cfg', 'gx'), 'gy'), parts along dimension 1
- new_link: float32 [12, 256, 16, 1024], P(None, ('cfg', 'gx'), 'gy'), parts along dimension 1
There are 2 independent parts, one for each index of `cfg`. A program takes and returns all parts, laid end to end along the dimension named above; each array names one. Nothing has to cross between parts.
Inputs may be any that keep to these rules, and one draw needn't show every extreme that they name: `gauge_links`: for every direction and site the two rows are orthonormal complex 3-vectors up to rounding.
All inputs are finite; a program needn't handle non-finite values.
Results may differ from a plain program's by a relative error of at most 0.0003.
Values sent between devices are 32-bit elements; how exact they have to be, the bound alone decides.
A program may use at most 128 MiB of HBM per device.

v0:
```python
import functools
import math

import jax
import jax.numpy as jnp
import numpy as np
from jax import lax
from jax.experimental import pallas as pl
from jax.experimental.pallas import tpu as pltpu
from jax.sharding import PartitionSpec as P

NZ = 32
NT = 32
LANES = 128

coupling = 6.0
step_force = 0.3
step_link = 0.15
kernel_mass = 0.01

f32 = jnp.float32
bf16 = jnp.bfloat16
VMEM = pl.BlockSpec(memory_space=pltpu.VMEM)
PARAMS = dict(vmem_limit_bytes=60 * 1024 * 1024)


def hartley(length):
    index = np.arange(length)
    angle = 2.0 * np.pi * (np.outer(index, index) % length) / length
    return np.cos(angle) + np.sin(angle)


def in_two(table):
    high = jnp.asarray(table, f32).astype(bf16)
    return high, (jnp.asarray(table, f32) - high.astype(f32)).astype(bf16)


def cdot(lefts, rights, conj_left=False, conj_right=False):
    re = im = None
    for (a, b), (c, d) in zip(lefts, rights):
        same = conj_left == conj_right
        re_term = a * c - b * d if same else a * c + b * d
        if not conj_left and not conj_right:
            im_term = a * d + b * c
        elif conj_left and not conj_right:
            im_term = a * d - b * c
        elif conj_right and not conj_left:
            im_term = b * c - a * d
        else:
            im_term = -(a * d + b * c)
        re = re_term if re is None else re + re_term
        im = im_term if im is None else im + im_term
    return re, im


def product(left, right, adj_left=False, adj_right=False):
    out = []
    for r in range(3):
        row = []
        lefts = [left[k][r] for k in range(3)] if adj_left else [left[r][k] for k in range(3)]
        for c in range(3):
            rights = [right[c][k] for k in range(3)] if adj_right else [right[k][c] for k in range(3)]
            row.append(cdot(lefts, rights, adj_left, adj_right))
        out.append(row)
    return out


def with_third(rows):
    third = []
    for k in range(3):
        i, j = (k + 1) % 3, (k + 2) % 3
        (a, b), (c, d) = rows[0][i], rows[1][j]
        (e, f), (g, h) = rows[0][j], rows[1][i]
        third.append(((a * c - b * d) - (e * g - f * h), (e * h + f * g) - (a * d + b * c)))
    return [rows[0], rows[1], third]


def matrix_of(get):
    return with_third([[(get(3 * r + k), get(6 + 3 * r + k)) for k in range(3)] for r in range(2)])


def algebra_parts(m):
    inv_root = 1.0 / math.sqrt(3.0)
    return [
        m[1][0][1] + m[0][1][1],
        m[0][1][0] - m[1][0][0],
        m[0][0][1] - m[1][1][1],
        m[2][0][1] + m[0][2][1],
        m[0][2][0] - m[2][0][0],
        m[2][1][1] + m[1][2][1],
        m[1][2][0] - m[2][1][0],
        (m[0][0][1] + m[1][1][1] - 2.0 * m[2][2][1]) * inv_root,
    ]


def split_dot(value, high_ref, low_ref, columns):
    high = value.astype(bf16)
    low = (value - high.astype(f32)).astype(bf16)
    table = high_ref[:, columns]
    return (
        jnp.dot(high, table, preferred_element_type=f32)
        + jnp.dot(low, table, preferred_element_type=f32)
        + jnp.dot(high, low_ref[:, columns], preferred_element_type=f32)
    )


def table_kernel(within_ref, across_ref, high_ref, low_ref):
    def block(z, carry):
        full = within_ref[...] * across_ref[pl.ds(z, 1), :]
        high = full.astype(bf16)
        rows = pl.ds(pl.multiple_of(z * NT, NT), NT)
        high_ref[rows, :] = high
        low_ref[rows, :] = (full - high.astype(f32)).astype(bf16)
        return carry

    lax.fori_loop(0, NZ, block, 0)


def plane_tables():
    sites = NZ * NT
    within = np.tile(hartley(NT), (1, NZ)).astype(np.float32)
    across = np.repeat(hartley(NZ), NT, axis=1).astype(np.float32)
    return pl.pallas_call(
        table_kernel,
        out_shape=[jax.ShapeDtypeStruct((sites, sites), bf16)] * 2,
        in_specs=[VMEM] * 2,
        out_specs=[VMEM] * 2,
        cost_estimate=pl.CostEstimate(flops=4 * sites * sites, bytes_accessed=8 * sites * sites, transcendentals=0),
        compiler_params=pltpu.CompilerParams(**PARAMS),
        name="plane_tables",
    )(jnp.asarray(within), jnp.asarray(across))


def force_kernel(
    links_ref, ahead_ref, rows_ref, corner_ref, momentum_ref, high_ref, low_ref,
    new_ref, spectrum_ref, partial_ref, staple_ref, behind_ref, edge_ref,
):
    tiles = new_ref.shape[2] // LANES
    lane = lax.broadcasted_iota(jnp.int32, (8, LANES), 1)
    sublane = lax.broadcasted_iota(jnp.int32, (8, LANES), 0)
    t_site = lane % NT

    edge_x = matrix_of(lambda e: rows_ref[12 + e])
    edge_y = matrix_of(lambda e: rows_ref[24 + e])
    edge_ahead = matrix_of(lambda e: corner_ref[e])
    edge = product(product(edge_x, edge_ahead), edge_y, adj_left=True)
    for r in range(3):
        for k in range(3):
            edge_ref[3 * r + k] = edge[r][k][0]
            edge_ref[9 + 3 * r + k] = edge[r][k][1]

    def first(i, carry):
        here = pl.ds(pl.multiple_of(i * LANES, LANES), LANES)
        after = pl.ds(pl.multiple_of(lax.rem(i + 1, tiles) * LANES, LANES), LANES)
        link_x = matrix_of(lambda e: links_ref[0, e, :, here])

        def moved_y(e):
            top = jnp.broadcast_to(rows_ref[e, pl.ds(i, 1), :], (8, LANES))
            return jnp.where(sublane == 7, top, pltpu.roll(links_ref[0, e, :, here], 7, 0))

        def moved_z(e):
            return jnp.where(
                lane < LANES - NT,
                pltpu.roll(links_ref[0, e, :, here], LANES - NT, 1),
                pltpu.roll(links_ref[0, e, :, after], LANES - NT, 1),
            )

        def moved_t(e):
            value = links_ref[0, e, :, here]
            return jnp.where(
                t_site == NT - 1, pltpu.roll(value, NT - 1, 1), pltpu.roll(value, LANES - 1, 1)
            )

        totals = None
        sums = None
        for nu, moved in ((1, moved_y), (2, moved_z), (3, moved_t)):
            link_nu = matrix_of(lambda e: links_ref[nu, e, :, here])
            ahead = matrix_of(lambda e: ahead_ref[nu - 1, e, :, here])
            path = product(link_x, ahead)
            lower = product(path, link_nu, adj_left=True)
            upper = product(path, product(link_nu, matrix_of(moved)), adj_right=True)
            parts = algebra_parts(upper)
            totals = parts if totals is None else [a + b for a, b in zip(totals, parts)]
            flat = [lower[r][k][p] for p in range(2) for r in range(3) for k in range(3)]
            if nu == 2:
                for e in range(18):
                    behind_ref[e, :, here] = flat[e]
                continue
            if nu == 1:
                flat = [
                    jnp.where(
                        sublane == 0,
                        jnp.broadcast_to(edge_ref[e, pl.ds(i, 1), :], (8, LANES)),
                        pltpu.roll(flat[e], 1, 0),
                    )
                    for e in range(18)
                ]
            else:
                flat = [
                    jnp.where(t_site == 0, pltpu.roll(v, LANES - NT + 1, 1), pltpu.roll(v, 1, 1))
                    for v in flat
                ]
            sums = flat if sums is None else [a + b for a, b in zip(sums, flat)]
        for e in range(18):
            staple_ref[e, :, here] = sums[e]
        for a in range(8):
            partial_ref[a, :, here] = totals[a]
        return carry

    lax.fori_loop(0, tiles, first, 0)

    def second(i, carry):
        here = pl.ds(pl.multiple_of(i * LANES, LANES), LANES)
        before = pl.ds(pl.multiple_of(lax.rem(i + tiles - 1, tiles) * LANES, LANES), LANES)
        flat = [
            staple_ref[e, :, here]
            + jnp.where(
                lane >= NT,
                pltpu.roll(behind_ref[e, :, here], NT, 1),
                pltpu.roll(behind_ref[e, :, before], NT, 1),
            )
            for e in range(18)
        ]
        staple = [[(flat[3 * r + k], flat[9 + 3 * r + k]) for k in range(3)] for r in range(3)]
        link_x = matrix_of(lambda e: links_ref[0, e, :, here])
        parts = algebra_parts(product(link_x, staple))
        for a in range(8):
            force = (coupling / 6.0) * (partial_ref[a, :, here] + parts[a])
            new_ref[a, :, here] = momentum_ref[a, :, here] - step_force * force
        return carry

    lax.fori_loop(0, tiles, second, 0)

    count = new_ref.shape[0] * new_ref.shape[1]
    half = tiles // 2
    value = new_ref[...].reshape(count, tiles * LANES)
    for pair in range(tiles // 2):
        columns = slice(pair * 2 * LANES, (pair + 1) * 2 * LANES)
        out = split_dot(value, high_ref, low_ref, columns)
        for side in range(2):
            tile = 2 * pair + side
            spectrum_ref[tile // half, pl.ds(tile % half, count, stride=half), :] = out[
                :, side * LANES : (side + 1) * LANES
            ]


def finish_kernel(filtered_ref, links_ref, high_ref, low_ref, new_ref, smooth_ref):
    tiles = new_ref.shape[2] // LANES
    half = tiles // 2
    count = 64
    pieces = [
        filtered_ref[tile // half, pl.ds(tile % half, count, stride=half), :] for tile in range(tiles)
    ]
    value = jnp.concatenate(pieces, axis=1)
    for pair in range(tiles // 2):
        columns = slice(pair * 2 * LANES, (pair + 1) * 2 * LANES)
        smooth_ref[:, columns] = split_dot(value, high_ref, low_ref, columns)
    root_inv = 1.0 / math.sqrt(3.0)
    scale = 0.25 * step_link * 0.5

    def one(i, carry):
        here = pl.ds(pl.multiple_of(i * LANES, LANES), LANES)
        s = [smooth_ref[pl.ds(8 * a, 8), here] * scale for a in range(8)]
        eighth = root_inv * s[7]
        h00, h11, h22 = eighth + s[2], eighth - s[2], -2.0 * eighth
        a01, b01 = s[0], -s[1]
        a02, b02 = s[3], -s[4]
        a12, b12 = s[5], -s[6]
        n01 = a01 * a01 + b01 * b01
        n02 = a02 * a02 + b02 * b02
        n12 = a12 * a12 + b12 * b12
        p = 0.5 * (h00 * h00 + h11 * h11 + h22 * h22) + (n01 + n02 + n12)
        m_re = a01 * a12 - b01 * b12
        m_im = a01 * b12 + b01 * a12
        q = h00 * h11 * h22 + 2.0 * (m_re * a02 + m_im * b02) - h00 * n12 - h11 * n02 - h22 * n01
        pq = p * q
        pp = p * p
        c0 = (1.0 - q * q * (1.0 / 720.0), pq * (1.0 / 120.0) - q * (1.0 / 6.0))
        c1 = (q * (1.0 / 24.0) - pq * (1.0 / 360.0), 1.0 - p * (1.0 / 6.0) + pp * (1.0 / 120.0))
        c2 = (p * (1.0 / 24.0) - 0.5 - pp * (1.0 / 720.0), q * (1.0 / 120.0))

        def cm(u, v):
            return (u[0] * v[0] - u[1] * v[1], u[0] * v[1] + u[1] * v[0])

        for _ in range(2):
            s00, s11, s22 = cm(c0, c0), cm(c1, c1), cm(c2, c2)
            d01, d02, d12 = cm(c0, c1), cm(c0, c2), cm(c1, c2)
            c0, c1, c2 = (
                tuple(s00[x] + 2.0 * q * d12[x] for x in range(2)),
                tuple(2.0 * (d01[x] + p * d12[x]) + q * s22[x] for x in range(2)),
                tuple(2.0 * d02[x] + s11[x] + p * s22[x] for x in range(2)),
            )
        g00 = h00 * h00 + n01 + n02
        g11 = h11 * h11 + n01 + n12
        g01 = (a01 * (h00 + h11) + a02 * a12 + b02 * b12, b01 * (h00 + h11) + b02 * a12 - a02 * b12)
        g02 = (a02 * (h00 + h22) + m_re, b02 * (h00 + h22) + m_im)
        g12 = (a12 * (h11 + h22) + a01 * a02 + b01 * b02, b12 * (h11 + h22) + a01 * b02 - b01 * a02)

        def mix(h, g):
            first, second = cm(c1, h), cm(c2, g)
            return (first[0] + second[0], first[1] + second[1])

        def diagonal(h, g):
            return (c0[0] + c1[0] * h + c2[0] * g, c0[1] + c1[1] * h + c2[1] * g)

        rotation = [
            [diagonal(h00, g00), mix((a01, b01), g01), mix((a02, b02), g02)],
            [mix((a01, -b01), (g01[0], -g01[1])), diagonal(h11, g11), mix((a12, b12), g12)],
        ]
        link = matrix_of(lambda e: links_ref[e, :, here])
        for r in range(2):
            for k in range(3):
                re, im = cdot(rotation[r], [link[m][k] for m in range(3)])
                new_ref[3 * r + k, :, here] = re
                new_ref[6 + 3 * r + k, :, here] = im
        return carry

    lax.fori_loop(0, tiles, one, 0)


def filter_kernel(
    inner, outer, y_table,
    spectrum_ref, weight_ref, high_ref, low_ref, out_ref,
    both_ref, bands_ref, arrive_ref, whole_ref, done_ref, back_ref, rows_ref, halves_ref,
    pair_sems, inner_sems, outer_sems, outer_back_sems, inner_back_sems, pair_back_sems,
):
    me = lax.axis_index("gx")
    core = lax.axis_index("gy")
    other = 1 - core
    row = me // inner
    col = me % inner

    def at_col(d):
        return lax.rem(col + d, inner)

    def at_row(d):
        return lax.rem(row + d, outer)

    barrier = pltpu.get_barrier_semaphore()

    def greet_col(d, carry):
        pl.semaphore_signal(barrier, inc=1, device_id={"gx": row * inner + at_col(d)}, device_id_type=pl.DeviceIdType.MESH)
        return carry

    def greet_row(d, carry):
        pl.semaphore_signal(barrier, inc=1, device_id={"gx": at_row(d) * inner + col}, device_id_type=pl.DeviceIdType.MESH)
        return carry

    lax.fori_loop(1, inner, greet_col, 0)
    lax.fori_loop(1, outer, greet_row, 0)
    pl.semaphore_signal(barrier, inc=1, device_id={"gy": other}, device_id_type=pl.DeviceIdType.MESH)
    pl.semaphore_wait(barrier, inner + outer - 1)

    def exchange(count, sems, source, target, device, own):
        def copy(d):
            return pltpu.make_async_remote_copy(
                src_ref=source(d), dst_ref=target, send_sem=sems.at[0, d], recv_sem=sems.at[1, d],
                device_id=device(d), device_id_type=pl.DeviceIdType.MESH,
            )

        def begin(d, carry):
            copy(d).start()
            return carry

        def finish(d, carry):
            copy(d).wait()
            return carry

        lax.fori_loop(1, count, begin, 0)
        local = pltpu.make_async_copy(own, target, sems.at[0, 0])
        local.start()
        lax.fori_loop(1, count, finish, 0)
        local.wait()

    def partner(d):
        return {"gy": other}

    exchange(2, pair_sems, lambda d: spectrum_ref.at[other], both_ref.at[core], partner, spectrum_ref.at[core])
    local_y = both_ref.shape[2]
    total_y = 2 * local_y

    def forward_y(c, carry):
        lines = [both_ref[y // local_y, c, y % local_y] for y in range(total_y)]
        for k in range(total_y):
            total = None
            for y in range(total_y):
                term = float(y_table[k, y]) * lines[y]
                total = term if total is None else total + term
            bands_ref[k, c] = total
        return carry

    lax.fori_loop(0, outer, forward_y, 0)
    exchange(
        inner, inner_sems, lambda d: bands_ref.at[at_col(d)], arrive_ref.at[col],
        lambda d: {"gx": row * inner + at_col(d)}, bands_ref.at[col],
    )
    exchange(
        outer, outer_sems, lambda d: arrive_ref.at[:, at_row(d)], whole_ref.at[row],
        lambda d: {"gx": at_row(d) * inner + col}, arrive_ref.at[:, row],
    )

    shape = whole_ref.shape
    flat = (shape[0] * shape[1] * shape[2], shape[3])

    def transform(value):
        high = value.astype(bf16)
        low = (value - high.astype(f32)).astype(bf16)
        table = high_ref[...]
        return (
            jnp.dot(table, high, preferred_element_type=f32)
            + jnp.dot(table, low, preferred_element_type=f32)
            + jnp.dot(low_ref[...], high, preferred_element_type=f32)
        )

    value = transform(whole_ref[...].reshape(flat)) * weight_ref[...]
    done_ref[...] = transform(value).reshape(shape)

    exchange(
        outer, outer_back_sems, lambda d: done_ref.at[at_row(d)], back_ref.at[:, row],
        lambda d: {"gx": at_row(d) * inner + col}, done_ref.at[row],
    )
    exchange(
        inner, inner_back_sems, lambda d: back_ref.at[at_col(d)], rows_ref.at[col],
        lambda d: {"gx": row * inner + at_col(d)}, back_ref.at[col],
    )

    def inverse_y(c, carry):
        lines = [rows_ref[k, c] for k in range(total_y)]
        for y in range(total_y):
            total = None
            for k in range(total_y):
                term = float(y_table[k, y]) * lines[k]
                total = term if total is None else total + term
            halves_ref[y // local_y, c, y % local_y] = total
        return carry

    lax.fori_loop(0, outer, inverse_y, 0)
    exchange(2, pair_back_sems, lambda d: halves_ref.at[other], out_ref.at[core], partner, halves_ref.at[core])


def filtered_modes(spectrum, weights, x_high, x_low, inner, outer):
    halves, channels, local_y, lines, lanes = spectrum.shape
    band = (channels, lines, lanes)
    scratch = [
        pltpu.VMEM(spectrum.shape, f32),
        pltpu.VMEM((inner,) + band, f32),
        pltpu.VMEM((inner,) + band, f32),
        pltpu.VMEM((outer, inner, lines, lanes), f32),
        pltpu.VMEM((outer, inner, lines, lanes), f32),
        pltpu.VMEM((inner,) + band, f32),
        pltpu.VMEM((inner,) + band, f32),
        pltpu.VMEM(spectrum.shape, f32),
    ]
    sems = [pltpu.SemaphoreType.DMA((2, n)) for n in (2, inner, outer, outer, inner, 2)]
    return pl.pallas_call(
        functools.partial(filter_kernel, inner, outer, hartley(2 * local_y)),
        out_shape=jax.ShapeDtypeStruct(spectrum.shape, f32),
        in_specs=[VMEM] * 4,
        out_specs=VMEM,
        scratch_shapes=scratch + sems,
        compiler_params=pltpu.CompilerParams(collective_id=0, has_side_effects=True, **PARAMS),
        name="filter_modes",
    )(spectrum, weights, x_high, x_low)


def sine_squares(length):
    return np.sin(np.pi * np.arange(length) / length) ** 2


def mode_weights(x_total, y_total, lines):
    sites = NZ * NT
    modes = np.arange(sites)
    plane = sine_squares(NZ)[modes // NT] + sine_squares(NT)[modes % NT]
    plane = jnp.asarray(plane.reshape(2, lines, LANES), f32)[lax.axis_index("gy")]
    y_part = jnp.asarray(sine_squares(y_total), f32)[lax.axis_index("gx") % y_total]
    x_part = jnp.asarray(np.repeat(sine_squares(x_total), lines), f32)
    tiled = jnp.tile(plane, (x_total, 1))
    denom = kernel_mass + 4.0 * (x_part[:, None] + y_part + tiled)
    return (4.0 / (x_total * y_total * sites)) / denom


def shards(gauge_links, momentum):
    channels, _, local_y, sites = momentum.shape
    gx_count = lax.axis_size("gx")
    inner = 2 * local_y
    outer = channels
    lines = sites // LANES // 2
    links = gauge_links.reshape(4, 12, local_y, sites)

    ahead = lax.ppermute(links[1:4], "gx", [((i + 1) % gx_count, i) for i in range(gx_count)])
    bottom_y = links[1, :, local_y - 1]
    edge_rows = jnp.concatenate([links[0, :, 0], links[0, :, local_y - 1], bottom_y])
    edge_rows = lax.ppermute(edge_rows, "gy", [(0, 1), (1, 0)])
    corner = lax.ppermute(
        bottom_y, ("gx", "gy"),
        [(((i + 1) % gx_count) * 2 + 1 - g, i * 2 + g) for i in range(gx_count) for g in range(2)],
    )
    edge_rows = edge_rows.reshape(36, sites // LANES, LANES)
    corner = corner.reshape(12, sites // LANES, LANES)

    plane_high, plane_low = plane_tables()
    weights = mode_weights(gx_count, inner, lines)
    x_high, x_low = in_two(np.kron(hartley(gx_count), np.eye(lines)).astype(np.float32))

    new_momentum, spectrum = pl.pallas_call(
        force_kernel,
        out_shape=[
            jax.ShapeDtypeStruct((channels, local_y, sites), f32),
            jax.ShapeDtypeStruct((2, channels * local_y * lines, LANES), f32),
        ],
        in_specs=[VMEM] * 7,
        out_specs=[VMEM] * 2,
        scratch_shapes=[
            pltpu.VMEM((8, local_y, sites), f32),
            pltpu.VMEM((18, local_y, sites), f32),
            pltpu.VMEM((18, local_y, sites), f32),
            pltpu.VMEM((18, sites // LANES, LANES), f32),
        ],
        compiler_params=pltpu.CompilerParams(**PARAMS),
        name="force_and_plane",
    )(links, ahead, edge_rows, corner, momentum.reshape(channels, local_y, sites), plane_high, plane_low)

    spectrum = spectrum.reshape(2, channels, local_y, lines, LANES)
    filtered = filtered_modes(spectrum, weights, x_high, x_low, inner, outer)
    filtered = filtered.reshape(2, channels * local_y * lines, LANES)

    new_link = pl.pallas_call(
        finish_kernel,
        out_shape=jax.ShapeDtypeStruct((12, local_y, sites), f32),
        in_specs=[VMEM] * 4,
        out_specs=VMEM,
        scratch_shapes=[pltpu.VMEM((channels * local_y, sites), f32)],
        compiler_params=pltpu.CompilerParams(**PARAMS),
        name="link_update",
    )(filtered, links[0], plane_high, plane_low)
    return (new_momentum.reshape(momentum.shape), new_link.reshape(12, 1, local_y, sites))


def solution(mesh):
    return jax.shard_map(
        shards,
        mesh=mesh,
        in_specs=(P(None, None, ("cfg", "gx"), "gy", None), P(None, ("cfg", "gx"), "gy", None)),
        out_specs=(P(None, ("cfg", "gx"), "gy", None), P(None, ("cfg", "gx"), "gy", None)),
        check_vma=False,
    )
```

profile of v0, /device:TPU:65, one launch (start us, length us, event | category | flops | bytes accessed | tf_op | source)
XLA Modules:
  0.0 151.6 jit_solution(5500395836233797951)
XLA Ops:
  0.6 0.0 copy-start.3
  0.6 0.0 copy-start.2
  0.7 0.0 copy-start.1
  0.7 1.4 slice_bitcast_fusion
  2.0 47.8 %collective-permute-start = (f32[3,12,8,1024]{3,2,1,0:T(8,128)S(1)}, f32[3,12,8,1024]{3,2,1,0:T(8,128)S(1)}, u32[]{:S(2)}, u32[]{:S(2)}) collective-permute-start(f32[3,12,8,1024]{3,2,1,0:T(8,128)S(1)} %slice_bitcast_fusion), channel_id=1, source_target_pairs={{2,0},{4,2},{6,4},{8,6},{10,8},{12,10},{14,12},{16,14},{18,16},{20... | collective-permute-start | bytes 3538952 | tf_op jit(solution)/shard_map/ppermute | solution.py:490
  49.9 1.4 fusion
  51.2 2.4 %collective-permute-start.2 = (f32[12,1024]{1,0:T(8,128)S(1)}, f32[12,1024]{1,0:T(8,128)S(1)}, u32[]{:S(2)}, u32[]{:S(2)}) collective-permute-start(f32[12,1024]{1,0:T(8,128)S(1)} %bitcast.43), channel_id=1, source_target_pairs={{3,0},{2,1},{5,2},{4,3},{7,4},{6,5},{9,6},{8,7},{11,8},{10,9},{13,... | collective-permute-start | bytes 147464 | tf_op jit(solution)/shard_map/ppermute | solution.py:494
  53.7 2.3 %collective-permute-start.1 = (f32[36,1024]{1,0:T(8,128)S(1)}, f32[36,1024]{1,0:T(8,128)S(1)}, u32[]{:S(2)}, u32[]{:S(2)}) collective-permute-start(f32[36,1024]{1,0:T(8,128)S(1)} %pad_maximum_fusion), channel_id=1, source_target_pairs={{0,1},{1,0},{2,3},{3,2},{4,5},{5,4},{6,7},{7,6},{8,9},{9,8},{10,11... | collective-permute-start | bytes 442376 | tf_op jit(solution)/shard_map/ppermute | solution.py:493
  56.1 0.0 copy-done.3
  56.1 0.6 dynamic_slice.6
  56.7 0.0 copy-done.2
  56.7 0.6 broadcast_add_fusion
  57.4 1.8 %slice_bitcast_fusion.1.links_ref = f32[12,8,1024]{2,1,0:T(8,128)} fusion(f32[4,12,1,8,1024]{4,3,1,2,0:T(8,128)} %bitcast.35), kind=kLoop, calls=%fused_computation.1 | loop fusion | bytes 786432 | tf_op jit(solution)/shard_map/squeeze | solution.py:535
  59.2 0.9 add_divide_fusion.weight_ref
  60.1 3.8 %plane_tables.1 = (bf16[1024,1024]{1,0:T(8,128)(2,1)}, bf16[1024,1024]{1,0:T(8,128)(2,1)}) custom-call(f32[32,1024]{1,0:T(8,128)} %constant.42.clone.within_ref, f32[32,1024]{1,0:T(8,128)} %constant.43.clone.across_ref), custom_call_target="tpu_custom_call" | custom-call | flops 4194304 | bytes 8388608 | tf_op jit(solution)/shard_map/plane_tables/pallas_call | solution.py:123
  63.9 12.1 %collective-permute-done.2 = f32[12,1024]{1,0:T(8,128)S(1)} collective-permute-done((f32[12,1024]{1,0:T(8,128)S(1)}, f32[12,1024]{1,0:T(8,128)S(1)}, u32[]{:S(2)}, u32[]{:S(2)}) %collective-permute-start.2) | collective-permute-done | bytes 49184 | tf_op jit(solution)/shard_map/ppermute | solution.py:494
  76.0 0.6 slice.31.corner_ref
  76.6 0.0 collective-permute-done.1
  76.6 0.7 slice.30.rows_ref
  77.3 0.0 collective-permute-done.ahead_ref
  77.3 1.0 copy-done
  78.3 9.5 %force_and_plane.1 = (f32[8,8,1024]{2,1,0:T(8,128)}, f32[2,256,128]{2,1,0:T(8,128)}) custom-call(f32[4,12,8,1024]{3,2,1,0:T(8,128)} %bitcast.36, f32[3,12,8,1024]{3,2,1,0:T(8,128)} %copy-done, f32[36,8,128]{2,1,0:T(8,128)} %slice.30.rows_ref, f32[12,8,128]{2,1,0:T(8,128)} %slice.31.corner_ref, f32[8,8,1024]{2,1,0:T(8,128)} %bitcast.41, ...), custom_call_target="tpu_custom_call" | custom-call | tf_op jit(solution)/shard_map/force_and_plane/pallas_call | solution.py:505
  87.9 58.7 %filter_modes.1 = f32[2,8,8,4,128]{4,3,2,1,0:T(4,128)} custom-call(f32[2,8,8,4,128]{4,3,2,1,0:T(4,128)} %bitcast.42, f32[512,128]{1,0:T(8,128)} %add_divide_fusion.weight_ref, bf16[512,512]{1,0:T(8,128)(2,1)} %constant.50.high_ref, bf16[512,512]{1,0:T(8,128)(2,1)} %constant.53.low_ref), custom_call_target="tpu_custom_call" | custom-call | tf_op jit(solution)/shard_map/filter_modes/pallas_call | solution.py:455
  146.6 5.0 %link_update.1 = f32[12,8,1024]{2,1,0:T(8,128)} custom-call(f32[2,256,128]{2,1,0:T(8,128)} %bitcast.37, f32[12,8,1024]{2,1,0:T(8,128)} %slice_bitcast_fusion.1.links_ref, bf16[1024,1024]{1,0:T(8,128)(2,1)} %get-tuple-element.6.high_ref, bf16[1024,1024]{1,0:T(8,128)(2,1)} %get-tuple-element.7.low_ref), custom_call_target="tpu_custom_call" | custom-call | tf_op jit(solution)/shard_map/link_update/pallas_call | solution.py:527
  (9 shorter events, 0.1 us)
Async XLA Ops:
  0.6 55.5 %copy-start.3 = (f32[16]{0:T(128)S(1)}, f32[16]{0:T(128)}, u32[]{:S(2)}) copy-start(f32[16]{0:T(128)} %constant.45.clone) | copy-start | bytes 196
  0.6 56.1 %copy-start.2 = (f32[2,4,128]{2,1,0:T(4,128)S(1)}, f32[2,4,128]{2,1,0:T(4,128)}, u32[]{:S(2)}) copy-start(f32[2,4,128]{2,1,0:T(4,128)} %constant.44.clone) | copy-start | bytes 12292
  0.7 56.0 %copy-start.1 = (f32[512]{0:T(512)S(1)}, f32[512]{0:T(512)}, u32[]{:S(2)}) copy-start(f32[512]{0:T(512)} %constant.46.clone) | copy-start | bytes 6148
  2.0 75.3 %collective-permute-start = (f32[3,12,8,1024]{3,2,1,0:T(8,128)S(1)}, f32[3,12,8,1024]{3,2,1,0:T(8,128)S(1)}, u32[]{:S(2)}, u32[]{:S(2)}) collective-permute-start(f32[3,12,8,1024]{3,2,1,0:T(8,128)S(1)} %slice_bitcast_fusion), channel_id=1, source_target_pairs={{2,0},{4,2},{6,4},{8,6},{10,8},{12,10},{14,12},{16,14},{18,16},{20... | collective-permute-start | bytes 3538952 | tf_op jit(solution)/shard_map/ppermute | solution.py:490
  51.2 24.7 %collective-permute-start.2 = (f32[12,1024]{1,0:T(8,128)S(1)}, f32[12,1024]{1,0:T(8,128)S(1)}, u32[]{:S(2)}, u32[]{:S(2)}) collective-permute-start(f32[12,1024]{1,0:T(8,128)S(1)} %bitcast.43), channel_id=1, source_target_pairs={{3,0},{2,1},{5,2},{4,3},{7,4},{6,5},{9,6},{8,7},{11,8},{10,9},{13,... | collective-permute-start | bytes 147464 | tf_op jit(solution)/shard_map/ppermute | solution.py:494
  53.7 22.9 %collective-permute-start.1 = (f32[36,1024]{1,0:T(8,128)S(1)}, f32[36,1024]{1,0:T(8,128)S(1)}, u32[]{:S(2)}, u32[]{:S(2)}) collective-permute-start(f32[36,1024]{1,0:T(8,128)S(1)} %pad_maximum_fusion), channel_id=1, source_target_pairs={{0,1},{1,0},{2,3},{3,2},{4,5},{5,4},{6,7},{7,6},{8,9},{9,8},{10,11... | collective-permute-start | bytes 442376 | tf_op jit(solution)/shard_map/ppermute | solution.py:493
  77.3 1.0 copy-start
where the time goes:
time: 152 us
  Pallas kernels  77 us (51%)
  starting transfers between devices  52.6 us (35%)
  waiting for transfers between devices  12.1 us (8%)
  local copies, waits for them, and re-layouts  7.55 us (5%)
  other arithmetic  1.53 us (1%)
    pallas_call x1, Pallas kernels, filtered_modes(): pl.pallas_call(functools.partial(filter_kernel, inner, outer, hartley(2 *...  58.7 us
    ppermute x1, starting transfers between devices, shards(): lax.ppermute(links[1:4], 'gx', [((i + 1) % gx_count, i) for i in range(gx...  47.8 us
    ppermute x1, waiting for transfers between devices, shards(): lax.ppermute(bottom_y, ('gx', 'gy'), [((i + 1) % gx_count * 2 + 1 - g, i...  12.1 us
    pallas_call x1, Pallas kernels, shards(): pl.pallas_call(force_kernel, out_shape=[jax.ShapeDtypeStruct((channels, l...  9.54 us
    pallas_call x1, Pallas kernels, shards(): pl.pallas_call(finish_kernel, out_shape=jax.ShapeDtypeStruct((12, local_y...  4.95 us
    pallas_call x1, Pallas kernels, plane_tables(): pl.pallas_call(table_kernel, out_shape=[jax.ShapeDtypeStruct((sites, site...  3.78 us
  transfers between devices with their start and end apart: 3, of which 1 were waited for; matrix products, arithmetic and copies ran while one was open for 4% of the time, Pallas kernels for 2%

commit v1 on v0

v1 whole, which is shorter than its diff:
```python
import functools
import math

import jax
import jax.numpy as jnp
import numpy as np
from jax import lax
from jax.experimental import pallas as pl
from jax.experimental.pallas import tpu as pltpu
from jax.sharding import PartitionSpec as P

NZ = 32
NT = 32
LANES = 128

coupling = 6.0
step_force = 0.3
step_link = 0.15
kernel_mass = 0.01

f32 = jnp.float32
bf16 = jnp.bfloat16
VMEM = pl.BlockSpec(memory_space=pltpu.VMEM)
PARAMS = dict(vmem_limit_bytes=60 * 1024 * 1024)


def hartley(length):
    index = np.arange(length)
    angle = 2.0 * np.pi * (np.outer(index, index) % length) / length
    return np.cos(angle) + np.sin(angle)


def in_two(table):
    high = jnp.asarray(table, f32).astype(bf16)
    return high, (jnp.asarray(table, f32) - high.astype(f32)).astype(bf16)


def cdot(lefts, rights, conj_left=False, conj_right=False):
    re = im = None
    for (a, b), (c, d) in zip(lefts, rights):
        same = conj_left == conj_right
        re_term = a * c - b * d if same else a * c + b * d
        if not conj_left and not conj_right:
            im_term = a * d + b * c
        elif conj_left and not conj_right:
            im_term = a * d - b * c
        elif conj_right and not conj_left:
            im_term = b * c - a * d
        else:
            im_term = -(a * d + b * c)
        re = re_term if re is None else re + re_term
        im = im_term if im is None else im + im_term
    return re, im


def product(left, right, adj_left=False, adj_right=False):
    out = []
    for r in range(3):
        row = []
        lefts = [left[k][r] for k in range(3)] if adj_left else [left[r][k] for k in range(3)]
        for c in range(3):
            rights = [right[c][k] for k in range(3)] if adj_right else [right[k][c] for k in range(3)]
            row.append(cdot(lefts, rights, adj_left, adj_right))
        out.append(row)
    return out


def with_third(rows):
    third = []
    for k in range(3):
        i, j = (k + 1) % 3, (k + 2) % 3
        (a, b), (c, d) = rows[0][i], rows[1][j]
        (e, f), (g, h) = rows[0][j], rows[1][i]
        third.append(((a * c - b * d) - (e * g - f * h), (e * h + f * g) - (a * d + b * c)))
    return [rows[0], rows[1], third]


def matrix_of(get):
    return with_third([[(get(3 * r + k), get(6 + 3 * r + k)) for k in range(3)] for r in range(2)])


def algebra_parts(m):
    inv_root = 1.0 / math.sqrt(3.0)
    return [
        m[1][0][1] + m[0][1][1],
        m[0][1][0] - m[1][0][0],
        m[0][0][1] - m[1][1][1],
        m[2][0][1] + m[0][2][1],
        m[0][2][0] - m[2][0][0],
        m[2][1][1] + m[1][2][1],
        m[1][2][0] - m[2][1][0],
        (m[0][0][1] + m[1][1][1] - 2.0 * m[2][2][1]) * inv_root,
    ]


def split_dot(value, high_ref, low_ref, columns):
    high = value.astype(bf16)
    low = (value - high.astype(f32)).astype(bf16)
    table = high_ref[:, columns]
    return (
        jnp.dot(high, table, preferred_element_type=f32)
        + jnp.dot(low, table, preferred_element_type=f32)
        + jnp.dot(high, low_ref[:, columns], preferred_element_type=f32)
    )


def finish_kernel(smooth_ref, links_ref, momentum_ref, new_ref, copied_ref):
    copied_ref[...] = momentum_ref[...]
    tiles = new_ref.shape[2] // LANES
    root_inv = 1.0 / math.sqrt(3.0)
    scale = 0.25 * step_link * 0.5

    def one(i, carry):
        here = pl.ds(pl.multiple_of(i * LANES, LANES), LANES)
        s = [smooth_ref[pl.ds(8 * a, 8), here] * scale for a in range(8)]
        eighth = root_inv * s[7]
        h00, h11, h22 = eighth + s[2], eighth - s[2], -2.0 * eighth
        a01, b01 = s[0], -s[1]
        a02, b02 = s[3], -s[4]
        a12, b12 = s[5], -s[6]
        n01 = a01 * a01 + b01 * b01
        n02 = a02 * a02 + b02 * b02
        n12 = a12 * a12 + b12 * b12
        p = 0.5 * (h00 * h00 + h11 * h11 + h22 * h22) + (n01 + n02 + n12)
        m_re = a01 * a12 - b01 * b12
        m_im = a01 * b12 + b01 * a12
        q = h00 * h11 * h22 + 2.0 * (m_re * a02 + m_im * b02) - h00 * n12 - h11 * n02 - h22 * n01
        pq = p * q
        pp = p * p
        c0 = (1.0 - q * q * (1.0 / 720.0), pq * (1.0 / 120.0) - q * (1.0 / 6.0))
        c1 = (q * (1.0 / 24.0) - pq * (1.0 / 360.0), 1.0 - p * (1.0 / 6.0) + pp * (1.0 / 120.0))
        c2 = (p * (1.0 / 24.0) - 0.5 - pp * (1.0 / 720.0), q * (1.0 / 120.0))

        def cm(u, v):
            return (u[0] * v[0] - u[1] * v[1], u[0] * v[1] + u[1] * v[0])

        for _ in range(2):
            s00, s11, s22 = cm(c0, c0), cm(c1, c1), cm(c2, c2)
            d01, d02, d12 = cm(c0, c1), cm(c0, c2), cm(c1, c2)
            c0, c1, c2 = (
                tuple(s00[x] + 2.0 * q * d12[x] for x in range(2)),
                tuple(2.0 * (d01[x] + p * d12[x]) + q * s22[x] for x in range(2)),
                tuple(2.0 * d02[x] + s11[x] + p * s22[x] for x in range(2)),
            )
        g00 = h00 * h00 + n01 + n02
        g11 = h11 * h11 + n01 + n12
        g01 = (a01 * (h00 + h11) + a02 * a12 + b02 * b12, b01 * (h00 + h11) + b02 * a12 - a02 * b12)
        g02 = (a02 * (h00 + h22) + m_re, b02 * (h00 + h22) + m_im)
        g12 = (a12 * (h11 + h22) + a01 * a02 + b01 * b02, b12 * (h11 + h22) + a01 * b02 - b01 * a02)

        def mix(h, g):
            first, second = cm(c1, h), cm(c2, g)
            return (first[0] + second[0], first[1] + second[1])

        def diagonal(h, g):
            return (c0[0] + c1[0] * h + c2[0] * g, c0[1] + c1[1] * h + c2[1] * g)

        rotation = [
            [diagonal(h00, g00), mix((a01, b01), g01), mix((a02, b02), g02)],
            [mix((a01, -b01), (g01[0], -g01[1])), diagonal(h11, g11), mix((a12, b12), g12)],
        ]
        link = matrix_of(lambda e: links_ref[0, e, :, here])
        for r in range(2):
            for k in range(3):
                re, im = cdot(rotation[r], [link[m][k] for m in range(3)])
                new_ref[3 * r + k, :, here] = re
                new_ref[6 + 3 * r + k, :, here] = im
        return carry

    lax.fori_loop(0, tiles, one, 0)


def step_kernel(
    inner, outer, y_table,
    links_hbm, momentum_hbm, plane_hbm, modes_hbm, x_hbm, y_squares,
    new_ref, smooth_ref,
    links_ref, ahead_ref, momentum_ref, plane_ref, modes_ref, x_ref,
    high_ref, low_ref, weight_ref, path_ref, partial_ref, staple_ref, behind_ref,
    top_out, top_in, edge_out, edge_in,
    spectrum_ref, both_ref, bands_ref, whole_ref, done_ref, back_ref, halves_ref, filtered_ref,
    load_sems, halo_sems, swap_sems, all_sems, ring_sems,
):
    me = lax.axis_index("gx")
    core = lax.axis_index("gy")
    other = 1 - core
    peers = inner * outer
    row = me // inner
    col = me % inner
    mesh_id = pl.DeviceIdType.MESH
    before = {"gx": lax.rem(me + peers - 1, peers)}
    after = {"gx": lax.rem(me + 1, peers)}
    partner = {"gy": other}
    col_before = {"gx": row * inner + lax.rem(col + inner - 1, inner)}
    col_after = {"gx": row * inner + lax.rem(col + 1, inner)}
    row_before = {"gx": lax.rem(row + outer - 1, outer) * inner + col}
    row_after = {"gx": lax.rem(row + 1, outer) * inner + col}
    neighbours = (before, after, partner, col_before, col_after, row_before, row_after)

    def signal(sem, device):
        pl.semaphore_signal(sem, inc=1, device_id=device, device_id_type=mesh_id)

    def send(source, target, sems, device):
        return pltpu.make_async_remote_copy(
            src_ref=source, dst_ref=target, send_sem=sems.at[0], recv_sem=sems.at[1],
            device_id=device, device_id_type=mesh_id,
        )

    barrier = pltpu.get_barrier_semaphore()
    for device in neighbours:
        signal(barrier, device)
    loads = [
        pltpu.make_async_copy(links_hbm, links_ref, load_sems.at[0]),
        pltpu.make_async_copy(plane_hbm, plane_ref, load_sems.at[1]),
        pltpu.make_async_copy(modes_hbm.at[core], modes_ref, load_sems.at[2]),
        pltpu.make_async_copy(x_hbm, x_ref, load_sems.at[3]),
        pltpu.make_async_copy(momentum_hbm, momentum_ref, load_sems.at[4]),
    ]
    for load in loads:
        load.start()
    pl.semaphore_wait(barrier, len(neighbours))

    halos = [send(links_hbm.at[nu], ahead_ref.at[nu - 1], halo_sems.at[nu - 1], before) for nu in (1, 2, 3)]
    for halo in halos:
        halo.start()

    def relay(steps, behind, ahead, first):
        def step(k, carry):
            signal(ring_sems.at[first], ahead)
            signal(ring_sems.at[first + 1], behind)
            pl.semaphore_wait(ring_sems.at[first], 1)
            pl.semaphore_wait(ring_sems.at[first + 1], 1)
            return carry

        lax.fori_loop(0, steps, step, 0)

    tiles = new_ref.shape[2] // LANES
    lane = lax.broadcasted_iota(jnp.int32, (8, LANES), 1)
    sublane = lax.broadcasted_iota(jnp.int32, (8, LANES), 0)
    t_site = lane % NT

    def lanes_of(i):
        return pl.ds(pl.multiple_of(i * LANES, LANES), LANES)

    loads[0].wait()

    def pack_top(i, carry):
        for e in range(12):
            top_out[e, pl.ds(i, 1), :] = links_ref[0, e, 0:1, lanes_of(i)]
        return carry

    lax.fori_loop(0, tiles, pack_top, 0)
    top = send(top_out, top_in, halo_sems.at[3], partner)
    top.start()
    relay(inner // 2, col_before, col_after, 0)
    relay(outer // 2, row_before, row_after, 2)

    for load in loads[1:]:
        load.wait()

    def table_block(z, carry):
        full = plane_ref[0] * plane_ref[1, pl.ds(z, 1), :]
        high = full.astype(bf16)
        rows = pl.ds(pl.multiple_of(z * NT, NT), NT)
        high_ref[rows, :] = high
        low_ref[rows, :] = (full - high.astype(f32)).astype(bf16)
        return carry

    lax.fori_loop(0, NZ, table_block, 0)
    scale = 4.0 / (peers * inner * NZ * NT)
    weight_ref[...] = scale / (kernel_mass + 4.0 * (modes_ref[...] + y_squares[col]))
    top.wait()

    def prepare(i, carry):
        here = lanes_of(i)
        following = lanes_of(lax.rem(i + 1, tiles))

        def moved_y(e):
            edge = jnp.broadcast_to(top_in[e, pl.ds(i, 1), :], (8, LANES))
            return jnp.where(sublane == 7, edge, pltpu.roll(links_ref[0, e, :, here], 7, 0))

        def moved_z(e):
            return jnp.where(
                lane < LANES - NT,
                pltpu.roll(links_ref[0, e, :, here], LANES - NT, 1),
                pltpu.roll(links_ref[0, e, :, following], LANES - NT, 1),
            )

        def moved_t(e):
            value = links_ref[0, e, :, here]
            return jnp.where(
                t_site == NT - 1, pltpu.roll(value, NT - 1, 1), pltpu.roll(value, LANES - 1, 1)
            )

        for nu, moved in ((1, moved_y), (2, moved_z), (3, moved_t)):
            link_nu = matrix_of(lambda e: links_ref[nu, e, :, here])
            path = product(link_nu, matrix_of(moved))
            for r in range(3):
                for k in range(3):
                    path_ref[nu - 1, 3 * r + k, :, here] = path[r][k][0]
                    path_ref[nu - 1, 9 + 3 * r + k, :, here] = path[r][k][1]
        return carry

    lax.fori_loop(0, tiles, prepare, 0)

    def staples(nu, i):
        here = lanes_of(i)
        link_x = matrix_of(lambda e: links_ref[0, e, :, here])
        link_nu = matrix_of(lambda e: links_ref[nu, e, :, here])
        ahead = matrix_of(lambda e: ahead_ref[nu - 1, e, :, here])
        corner = product(link_x, ahead)
        lower = product(corner, link_nu, adj_left=True)
        path = [
            [(path_ref[nu - 1, 3 * r + k, :, here], path_ref[nu - 1, 9 + 3 * r + k, :, here]) for k in range(3)]
            for r in range(3)
        ]
        parts = algebra_parts(product(corner, path, adj_right=True))
        for a in range(8):
            if nu == 1:
                partial_ref[a, :, here] = parts[a]
            else:
                partial_ref[a, :, here] += parts[a]
        return here, [lower[r][k][p] for p in range(2) for r in range(3) for k in range(3)]

    def along_y(i, carry):
        here, flat = staples(1, i)
        for e in range(18):
            edge_out[e, pl.ds(i, 1), :] = flat[e][7:8, :]
            staple_ref[e, :, here] = jnp.where(sublane == 0, 0.0, pltpu.roll(flat[e], 1, 0))
        return carry

    def along_z(i, carry):
        here, flat = staples(2, i)
        for e in range(18):
            behind_ref[e, :, here] = flat[e]
        return carry

    def along_t(i, carry):
        here, flat = staples(3, i)
        for e in range(18):
            staple_ref[e, :, here] += jnp.where(
                t_site == 0, pltpu.roll(flat[e], LANES - NT + 1, 1), pltpu.roll(flat[e], 1, 1)
            )
        return carry

    halos[0].wait_recv()
    lax.fori_loop(0, tiles, along_y, 0)
    edge = send(edge_out, edge_in, halo_sems.at[4], partner)
    edge.start()
    halos[1].wait_recv()
    lax.fori_loop(0, tiles, along_z, 0)
    halos[2].wait_recv()
    lax.fori_loop(0, tiles, along_t, 0)
    edge.wait()

    def force(i, carry):
        here = lanes_of(i)
        previous = lanes_of(lax.rem(i + tiles - 1, tiles))
        flat = [
            staple_ref[e, :, here]
            + jnp.where(sublane == 0, jnp.broadcast_to(edge_in[e, pl.ds(i, 1), :], (8, LANES)), 0.0)
            + jnp.where(
                lane >= NT,
                pltpu.roll(behind_ref[e, :, here], NT, 1),
                pltpu.roll(behind_ref[e, :, previous], NT, 1),
            )
            for e in range(18)
        ]
        staple = [[(flat[3 * r + k], flat[9 + 3 * r + k]) for k in range(3)] for r in range(3)]
        link_x = matrix_of(lambda e: links_ref[0, e, :, here])
        parts = algebra_parts(product(link_x, staple))
        for a in range(8):
            total = (coupling / 6.0) * (partial_ref[a, :, here] + parts[a])
            new_ref[a, :, here] = momentum_ref[a, :, here] - step_force * total
        return carry

    lax.fori_loop(0, tiles, force, 0)

    count = new_ref.shape[0] * new_ref.shape[1]
    half = tiles // 2
    value = new_ref[...].reshape(count, tiles * LANES)
    for pair in range(half):
        columns = slice(pair * 2 * LANES, (pair + 1) * 2 * LANES)
        out = split_dot(value, high_ref, low_ref, columns)
        for side in range(2):
            tile = 2 * pair + side
            spectrum_ref[tile // half, pl.ds(tile % half, count, stride=half), :] = out[
                :, side * LANES : (side + 1) * LANES
            ]

    def swap(source, target, stage):
        remote = send(source.at[other], target.at[core], swap_sems.at[stage], partner)
        remote.start()
        local = pltpu.make_async_copy(source.at[core], target.at[core], swap_sems.at[stage, 2])
        local.start()
        local.wait()
        remote.wait()

    def peer(d):
        step = (d + 1) // 2
        return lax.rem(me + lax.select(lax.rem(d, 2) == 1, step, peers - step), peers)

    def all_to_all(source, target, stage):
        def begin(d, carry):
            to = peer(d)
            send(source.at[to], target.at[me], all_sems.at[stage], {"gx": to}).start()
            return carry

        lax.fori_loop(1, peers, begin, 0)
        local = pltpu.make_async_copy(source.at[me], target.at[me], all_sems.at[stage, 2])
        local.start()
        local.wait()
        rest = pl.ds(0, peers - 1)
        pltpu.make_async_copy(source.at[rest], source.at[rest], all_sems.at[stage, 0]).wait()
        pltpu.make_async_copy(target.at[rest], target.at[rest], all_sems.at[stage, 1]).wait()

    swap(spectrum_ref, both_ref, 0)
    local_y = new_ref.shape[1]
    total_y = 2 * local_y

    def lines_of(c, y):
        return pl.ds(pl.multiple_of(c * (local_y * half), local_y * half) + (y % local_y) * half, half)

    def forward_y(c, carry):
        lines = [both_ref[y // local_y, lines_of(c, y), :] for y in range(total_y)]
        for k in range(total_y):
            total = None
            for y in range(total_y):
                term = float(y_table[k, y]) * lines[y]
                total = term if total is None else total + term
            bands_ref[c * inner + k] = total
        return carry

    lax.fori_loop(0, outer, forward_y, 0)
    all_to_all(bands_ref, whole_ref, 0)

    shape = whole_ref.shape
    flat_shape = (shape[0] * shape[1], shape[2])

    def transform(value):
        high = value.astype(bf16)
        low = (value - high.astype(f32)).astype(bf16)
        table = x_ref[0]
        return (
            jnp.dot(table, high, preferred_element_type=f32)
            + jnp.dot(table, low, preferred_element_type=f32)
            + jnp.dot(x_ref[1], high, preferred_element_type=f32)
        )

    modes = transform(whole_ref[...].reshape(flat_shape)) * weight_ref[...]
    done_ref[...] = transform(modes).reshape(shape)
    all_to_all(done_ref, back_ref, 1)

    def inverse_y(c, carry):
        lines = [back_ref[c * inner + k] for k in range(total_y)]
        for y in range(total_y):
            total = None
            for k in range(total_y):
                term = float(y_table[k, y]) * lines[k]
                total = term if total is None else total + term
            halves_ref[y // local_y, lines_of(c, y), :] = total
        return carry

    lax.fori_loop(0, outer, inverse_y, 0)
    swap(halves_ref, filtered_ref, 1)
    value = jnp.concatenate(
        [filtered_ref[tile // half, pl.ds(tile % half, count, stride=half), :] for tile in range(tiles)],
        axis=1,
    )
    for pair in range(half):
        columns = slice(pair * 2 * LANES, (pair + 1) * 2 * LANES)
        smooth_ref[:, columns] = split_dot(value, high_ref, low_ref, columns)
    for halo in halos:
        halo.wait_send()


def sine_squares(length):
    return np.sin(np.pi * np.arange(length) / length) ** 2


def shards(gauge_links, momentum):
    channels, _, local_y, sites = momentum.shape
    gx_count = lax.axis_size("gx")
    inner = 2 * local_y
    outer = channels
    tiles = sites // LANES
    half = tiles // 2
    rows = channels * local_y
    links = gauge_links.reshape(4, 12, local_y, sites)
    field = (channels, local_y, sites)

    plane = np.stack([np.tile(hartley(NT), (1, NZ)), np.repeat(hartley(NZ), NT, axis=1)]).astype(np.float32)
    index = np.arange(sites)
    z_t = (sine_squares(NZ)[index // NT] + sine_squares(NT)[index % NT]).reshape(2, half, LANES)
    modes = np.tile(z_t, (1, gx_count, 1)) + np.repeat(sine_squares(gx_count), half)[None, :, None]
    x_high, x_low = in_two(np.kron(hartley(gx_count), np.eye(half)).astype(np.float32))
    x_table = jnp.stack([x_high, x_low])
    y_squares = jnp.asarray(sine_squares(inner), f32)

    any_spec = pl.BlockSpec(memory_space=pl.ANY)
    exchanged = (gx_count, half, LANES)
    halved = (2, rows * half, LANES)
    staple = (18, local_y, sites)
    new_momentum, smooth = pl.pallas_call(
        functools.partial(step_kernel, inner, outer, hartley(inner)),
        out_shape=[jax.ShapeDtypeStruct(field, f32), jax.ShapeDtypeStruct((rows, sites), f32)],
        in_specs=[any_spec] * 5 + [pl.BlockSpec(memory_space=pltpu.SMEM)],
        out_specs=[VMEM] * 2,
        scratch_shapes=[
            pltpu.VMEM(links.shape, f32),
            pltpu.VMEM((3,) + links.shape[1:], f32),
            pltpu.VMEM(field, f32),
            pltpu.VMEM(plane.shape, f32),
            pltpu.VMEM(modes.shape[1:], f32),
            pltpu.VMEM(x_table.shape, bf16),
            pltpu.VMEM((sites, sites), bf16),
            pltpu.VMEM((sites, sites), bf16),
            pltpu.VMEM(modes.shape[1:], f32),
            pltpu.VMEM((3,) + staple, f32),
            pltpu.VMEM(field, f32),
            pltpu.VMEM(staple, f32),
            pltpu.VMEM(staple, f32),
            pltpu.VMEM((12, tiles, LANES), f32),
            pltpu.VMEM((12, tiles, LANES), f32),
            pltpu.VMEM((18, tiles, LANES), f32),
            pltpu.VMEM((18, tiles, LANES), f32),
            pltpu.VMEM(halved, f32),
            pltpu.VMEM(halved, f32),
            pltpu.VMEM(exchanged, f32),
            pltpu.VMEM(exchanged, f32),
            pltpu.VMEM(exchanged, f32),
            pltpu.VMEM(exchanged, f32),
            pltpu.VMEM(halved, f32),
            pltpu.VMEM(halved, f32),
            pltpu.SemaphoreType.DMA((5,)),
            pltpu.SemaphoreType.DMA((5, 2)),
            pltpu.SemaphoreType.DMA((2, 3)),
            pltpu.SemaphoreType.DMA((2, 3)),
            pltpu.SemaphoreType.REGULAR((4,)),
        ],
        compiler_params=pltpu.CompilerParams(collective_id=0, has_side_effects=True, **PARAMS),
        name="momentum_and_smooth",
    )(links, momentum.reshape(field), jnp.asarray(plane), jnp.asarray(modes, f32), x_table, y_squares)

    width = 2 * LANES
    new_link, new_momentum = pl.pallas_call(
        finish_kernel,
        grid=(sites // width,),
        out_shape=[jax.ShapeDtypeStruct(links.shape[1:], f32), jax.ShapeDtypeStruct(field, f32)],
        in_specs=[
            pl.BlockSpec((rows, width), lambda i: (0, i)),
            pl.BlockSpec((1, 12, local_y, width), lambda i: (0, 0, 0, i)),
            pl.BlockSpec((channels, local_y, width), lambda i: (0, 0, i)),
        ],
        out_specs=[
            pl.BlockSpec((12, local_y, width), lambda i: (0, 0, i)),
            pl.BlockSpec((channels, local_y, width), lambda i: (0, 0, i)),
        ],
        compiler_params=pltpu.CompilerParams(**PARAMS),
        name="link_update",
    )(smooth, links, new_momentum)
    return (new_momentum.reshape(momentum.shape), new_link.reshape(12, 1, local_y, sites))


def solution(mesh):
    return jax.shard_map(
        shards,
        mesh=mesh,
        in_specs=(P(None, None, ("cfg", "gx"), "gy", None), P(None, ("cfg", "gx"), "gy", None)),
        out_specs=(P(None, ("cfg", "gx"), "gy", None), P(None, ("cfg", "gx"), "gy", None)),
        check_vma=False,
    )
```

time: 152 us -> 126 us (0.83)
  starting transfers between devices: 52.6 us -> 0 us
  Pallas kernels: 77 us -> 125 us
  waiting for transfers between devices: 12.1 us -> 0 us
  local copies, waits for them, and re-layouts: 7.55 us -> 0 us
  other arithmetic: 1.53 us -> 0 us
    ppermute x3 -> x0, starting transfers between devices: 52.6 us -> none  [the longest x1 47.8 us: shards(): lax.ppermute(links[1:4], 'gx', [((i + 1) % gx_count, i) for i in range(gx...]
    pallas_call x4 -> x2, Pallas kernels: 77 us -> 125 us  [the longest x1 121 us: shards(): pl.pallas_call(functools.partial(step_kernel, inner, outer, hartley(inner...]
    ppermute x3 -> x0, waiting for transfers between devices: 12.1 us -> none  [the longest x1 12.1 us: shards(): lax.ppermute(bottom_y, ('gx', 'gy'), [((i + 1) % gx_count * 2 + 1 - g, i...]
    slice x2 -> x0, local copies, waits for them, and re-layouts: 2.71 us -> none  [the longest x1 1.36 us: shards(): links[1:4]]
    squeeze x2 -> x0, local copies, waits for them, and re-layouts: 1.84 us -> none  [the longest x1 1.82 us: shards(): links[0]]
  transfers between devices with their start and end apart: 3 -> 0, of which waited for: 1 -> 0; matrix products, arithmetic and copies ran while one was open for 4% -> 0% of each run, Pallas kernels for 2% -> 0%
where the time goes in v1:
time: 126 us; the launch traced here: 125 us
  Pallas kernels  125 us (99%)
    pallas_call x1, Pallas kernels, shards(): pl.pallas_call(functools.partial(step_kernel, inner, outer, hartley(inner...  121 us
    pallas_call x1, Pallas kernels, shards(): pl.pallas_call(finish_kernel, grid=(sites // width,), out_shape=[jax.Shap...  3.49 us

profile of v1, /device:TPU:65, one launch (start us, length us, event | category | flops | bytes accessed | tf_op | source)
XLA Modules:
  0.0 125.3 jit_solution(10326332128866190522)
XLA Ops:
  0.6 121.2 %momentum_and_smooth.1 = (f32[8,8,1024]{2,1,0:T(8,128)}, f32[64,1024]{1,0:T(8,128)}) custom-call(f32[4,12,8,1024]{3,2,1,0:T(8,128)} %bitcast.8, f32[8,8,1024]{2,1,0:T(8,128)} %bitcast.10, f32[2,32,1024]{2,1,0:T(8,128)} %constant.10.clone.plane_hbm, f32[2,512,128]{2,1,0:T(8,128)} %constant.11.clone.modes_hbm, bf16[2,512,512]{2,1,0:T(8,128)(2,1)} %constant.20.x_hbm, ...), custom_call_target="tpu_custom_call" | custom-call | tf_op jit(solution)/shard_map/momentum_and_smooth/pallas_call | solution.py:503
  121.8 3.5 %link_update.1 = (f32[12,8,1024]{2,1,0:T(8,128)}, f32[8,8,1024]{2,1,0:T(8,128)}) custom-call(f32[64,1024]{1,0:T(8,128)} %get-tuple-element.6.smooth_ref, f32[4,12,8,1024]{3,2,1,0:T(8,128)} %bitcast.9, f32[8,8,1024]{2,1,0:T(8,128)} %get-tuple-element.7.momentum_ref), custom_call_target="tpu_custom_call" | custom-call | tf_op jit(solution)/shard_map/link_update/pallas_call | solution.py:545

commit v2 on v1

--- a/solution.py
+++ b/solution.py
@@ -93,14 +93,14 @@
     ]
 
 
-def split_dot(value, high_ref, low_ref, columns):
+def split_dot(value, high_ref, low_ref, columns, rows=slice(None)):
     high = value.astype(bf16)
     low = (value - high.astype(f32)).astype(bf16)
-    table = high_ref[:, columns]
+    table = high_ref[rows, columns]
     return (
         jnp.dot(high, table, preferred_element_type=f32)
         + jnp.dot(low, table, preferred_element_type=f32)
-        + jnp.dot(high, low_ref[:, columns], preferred_element_type=f32)
+        + jnp.dot(high, low_ref[rows, columns], preferred_element_type=f32)
     )
 
 
@@ -177,7 +177,7 @@
     links_ref, ahead_ref, momentum_ref, plane_ref, modes_ref, x_ref,
     high_ref, low_ref, weight_ref, path_ref, partial_ref, staple_ref, behind_ref,
     top_out, top_in, edge_out, edge_in,
-    spectrum_ref, both_ref, bands_ref, whole_ref, done_ref, back_ref, halves_ref, filtered_ref,
+    plane_sum_ref, spectrum_ref, both_ref, bands_ref, whole_ref, done_ref, back_ref, halves_ref, filtered_ref,
     load_sems, halo_sems, swap_sems, all_sems, ring_sems,
 ):
     me = lax.axis_index("gx")
@@ -187,13 +187,25 @@
     row = me // inner
     col = me % inner
     mesh_id = pl.DeviceIdType.MESH
-    before = {"gx": lax.rem(me + peers - 1, peers)}
-    after = {"gx": lax.rem(me + 1, peers)}
-    partner = {"gy": other}
-    col_before = {"gx": row * inner + lax.rem(col + inner - 1, inner)}
-    col_after = {"gx": row * inner + lax.rem(col + 1, inner)}
-    row_before = {"gx": lax.rem(row + outer - 1, outer) * inner + col}
-    row_after = {"gx": lax.rem(row + 1, outer) * inner + col}
+    part = lax.axis_index("cfg")
+
+    def wrapped(value, count):
+        return lax.select(value >= count, value - count, value)
+
+    def at(place):
+        return (part, place, core)
+
+    def in_row(step):
+        return at(row * inner + wrapped(col + step % inner, inner))
+
+    def in_column(step):
+        return at(wrapped(row + step % outer, outer) * inner + col)
+
+    before = at(wrapped(me + peers - 1, peers))
+    after = at(wrapped(me + 1, peers))
+    partner = (part, me, other)
+    col_before, col_after = in_row(-1), in_row(1)
+    row_before, row_after = in_column(-1), in_column(1)
     neighbours = (before, after, partner, col_before, col_after, row_before, row_after)
 
     def signal(sem, device):
@@ -219,19 +231,27 @@
         load.start()
     pl.semaphore_wait(barrier, len(neighbours))
 
-    halos = [send(links_hbm.at[nu], ahead_ref.at[nu - 1], halo_sems.at[nu - 1], before) for nu in (1, 2, 3)]
+    sites = new_ref.shape[2]
+    halos = [send(links_hbm.at[nu], ahead_ref.at[nu - 1], halo_sems.at[nu - 1], before) for nu in (1, 2)]
+    quarters = 4
+    width = sites // quarters
+    for q in range(quarters):
+        lanes = pl.ds(q * width, width)
+        halos.append(
+            send(links_hbm.at[3, :, :, lanes], ahead_ref.at[2, :, :, lanes], halo_sems.at[2 + q], before)
+        )
     for halo in halos:
         halo.start()
 
-    def relay(steps, behind, ahead, first):
-        def step(k, carry):
-            signal(ring_sems.at[first], ahead)
-            signal(ring_sems.at[first + 1], behind)
-            pl.semaphore_wait(ring_sems.at[first], 1)
-            pl.semaphore_wait(ring_sems.at[first + 1], 1)
-            return carry
-
-        lax.fori_loop(0, steps, step, 0)
+    def relay(count, known, place, stage):
+        while known < count // 2:
+            distance = max(known, 1)
+            signal(ring_sems.at[stage], place(distance))
+            signal(ring_sems.at[stage], place(-distance))
+            pl.semaphore_wait(ring_sems.at[stage], 2)
+            known += distance
+            stage += 1
+        return stage
 
     tiles = new_ref.shape[2] // LANES
     lane = lax.broadcasted_iota(jnp.int32, (8, LANES), 1)
@@ -249,10 +269,8 @@
         return carry
 
     lax.fori_loop(0, tiles, pack_top, 0)
-    top = send(top_out, top_in, halo_sems.at[3], partner)
+    top = send(top_out, top_in, halo_sems.at[2 + quarters], partner)
     top.start()
-    relay(inner // 2, col_before, col_after, 0)
-    relay(outer // 2, row_before, row_after, 2)
 
     for load in loads[1:]:
         load.wait()
@@ -268,6 +286,8 @@
     lax.fori_loop(0, NZ, table_block, 0)
     scale = 4.0 / (peers * inner * NZ * NT)
     weight_ref[...] = scale / (kernel_mass + 4.0 * (modes_ref[...] + y_squares[col]))
+    last = relay(inner, 1, in_row, 0)
+    relay(outer, 0, in_column, last)
     top.wait()
 
     def prepare(i, carry):
@@ -344,12 +364,10 @@
 
     halos[0].wait_recv()
     lax.fori_loop(0, tiles, along_y, 0)
-    edge = send(edge_out, edge_in, halo_sems.at[4], partner)
+    edge = send(edge_out, edge_in, halo_sems.at[3 + quarters], partner)
     edge.start()
     halos[1].wait_recv()
     lax.fori_loop(0, tiles, along_z, 0)
-    halos[2].wait_recv()
-    lax.fori_loop(0, tiles, along_t, 0)
     edge.wait()
 
     def force(i, carry):
@@ -373,19 +391,28 @@
             new_ref[a, :, here] = momentum_ref[a, :, here] - step_force * total
         return carry
 
-    lax.fori_loop(0, tiles, force, 0)
-
     count = new_ref.shape[0] * new_ref.shape[1]
     half = tiles // 2
-    value = new_ref[...].reshape(count, tiles * LANES)
-    for pair in range(half):
-        columns = slice(pair * 2 * LANES, (pair + 1) * 2 * LANES)
-        out = split_dot(value, high_ref, low_ref, columns)
-        for side in range(2):
-            tile = 2 * pair + side
-            spectrum_ref[tile // half, pl.ds(tile % half, count, stride=half), :] = out[
-                :, side * LANES : (side + 1) * LANES
-            ]
+    per = tiles // quarters
+    for q in range(quarters):
+        halos[2 + q].wait_recv()
+        lax.fori_loop(per * q, per * (q + 1), along_t, 0)
+        lax.fori_loop(per * q, per * (q + 1), force, 0)
+        taken = slice(q * width, (q + 1) * width)
+        value = new_ref[:, :, taken].reshape(count, width)
+        for pair in range(half):
+            columns = slice(pair * 2 * LANES, (pair + 1) * 2 * LANES)
+            out = split_dot(value, high_ref, low_ref, columns, taken)
+            if q:
+                out = out + plane_sum_ref[:, columns]
+            if q < quarters - 1:
+                plane_sum_ref[:, columns] = out
+                continue
+            for side in range(2):
+                tile = 2 * pair + side
+                spectrum_ref[tile // half, pl.ds(tile % half, count, stride=half), :] = out[
+                    :, side * LANES : (side + 1) * LANES
+                ]
 
     def swap(source, target, stage):
         remote = send(source.at[other], target.at[core], swap_sems.at[stage], partner)
@@ -395,17 +422,17 @@
         local.wait()
         remote.wait()
 
-    def peer(d):
-        step = (d + 1) // 2
-        return lax.rem(me + lax.select(lax.rem(d, 2) == 1, step, peers - step), peers)
-
     def all_to_all(source, target, stage):
+        def push(to):
+            send(source.at[to], target.at[me], all_sems.at[stage], at(to)).start()
+
         def begin(d, carry):
-            to = peer(d)
-            send(source.at[to], target.at[me], all_sems.at[stage], {"gx": to}).start()
+            push(wrapped(me + d, peers))
+            push(wrapped(me + peers - d, peers))
             return carry
 
-        lax.fori_loop(1, peers, begin, 0)
+        lax.fori_loop(1, peers // 2, begin, 0)
+        push(wrapped(me + peers // 2, peers))
         local = pltpu.make_async_copy(source.at[me], target.at[me], all_sems.at[stage, 2])
         local.start()
         local.wait()
@@ -523,6 +550,7 @@
             pltpu.VMEM((12, tiles, LANES), f32),
             pltpu.VMEM((18, tiles, LANES), f32),
             pltpu.VMEM((18, tiles, LANES), f32),
+            pltpu.VMEM((rows, sites), f32),
             pltpu.VMEM(halved, f32),
             pltpu.VMEM(halved, f32),
             pltpu.VMEM(exchanged, f32),
@@ -532,10 +560,10 @@
             pltpu.VMEM(halved, f32),
             pltpu.VMEM(halved, f32),
             pltpu.SemaphoreType.DMA((5,)),
-            pltpu.SemaphoreType.DMA((5, 2)),
+            pltpu.SemaphoreType.DMA((8, 2)),
             pltpu.SemaphoreType.DMA((2, 3)),
             pltpu.SemaphoreType.DMA((2, 3)),
-            pltpu.SemaphoreType.REGULAR((4,)),
+            pltpu.SemaphoreType.REGULAR((2 * gx_count.bit_length(),)),
         ],
         compiler_params=pltpu.CompilerParams(collective_id=0, has_side_effects=True, **PARAMS),
         name="momentum_and_smooth",

time: 126 us -> 128 us (1.016)
  Pallas kernels: 125 us -> 127 us
    pallas_call x1, Pallas kernels: 121 us -> 124 us  [shards(): pl.pallas_call(functools.partial(step_kernel, inner, outer, hartley(inner...]
where the time goes in v2:
time: 128 us
  Pallas kernels  127 us (99%)
    pallas_call x1, Pallas kernels, shards(): pl.pallas_call(functools.partial(step_kernel, inner, outer, hartley(inner...  124 us
    pallas_call x1, Pallas kernels, shards(): pl.pallas_call(finish_kernel, grid=(sites // width,), out_shape=[jax.Shap...  3.49 us

profile of v2, /device:TPU:65, one launch (start us, length us, event | category | flops | bytes accessed | tf_op | source)
XLA Modules:
  0.0 128.0 jit_solution(9294420797626082262)
XLA Ops:
  0.6 123.8 %momentum_and_smooth.1 = (f32[8,8,1024]{2,1,0:T(8,128)}, f32[64,1024]{1,0:T(8,128)}) custom-call(f32[4,12,8,1024]{3,2,1,0:T(8,128)} %bitcast.8, f32[8,8,1024]{2,1,0:T(8,128)} %bitcast.10, f32[2,32,1024]{2,1,0:T(8,128)} %constant.10.clone.plane_hbm, f32[2,512,128]{2,1,0:T(8,128)} %constant.11.clone.modes_hbm, bf16[2,512,512]{2,1,0:T(8,128)(2,1)} %constant.20.x_hbm, ...), custom_call_target="tpu_custom_call" | custom-call | tf_op jit(solution)/shard_map/momentum_and_smooth/pallas_call | solution.py:530
  124.5 3.5 %link_update.1 = (f32[12,8,1024]{2,1,0:T(8,128)}, f32[8,8,1024]{2,1,0:T(8,128)}) custom-call(f32[64,1024]{1,0:T(8,128)} %get-tuple-element.6.smooth_ref, f32[4,12,8,1024]{3,2,1,0:T(8,128)} %bitcast.9, f32[8,8,1024]{2,1,0:T(8,128)} %get-tuple-element.7.momentum_ref), custom_call_target="tpu_custom_call" | custom-call | tf_op jit(solution)/shard_map/link_update/pallas_call | solution.py:573

commit v3 on v2

--- a/solution.py
+++ b/solution.py
@@ -243,15 +243,15 @@
     for halo in halos:
         halo.start()
 
-    def relay(count, known, place, stage):
-        while known < count // 2:
-            distance = max(known, 1)
-            signal(ring_sems.at[stage], place(distance))
-            signal(ring_sems.at[stage], place(-distance))
-            pl.semaphore_wait(ring_sems.at[stage], 2)
-            known += distance
-            stage += 1
-        return stage
+    def relay(steps, behind, ahead, first):
+        def step(k, carry):
+            signal(ring_sems.at[first], ahead)
+            signal(ring_sems.at[first + 1], behind)
+            pl.semaphore_wait(ring_sems.at[first], 1)
+            pl.semaphore_wait(ring_sems.at[first + 1], 1)
+            return carry
+
+        lax.fori_loop(0, steps, step, 0)
 
     tiles = new_ref.shape[2] // LANES
     lane = lax.broadcasted_iota(jnp.int32, (8, LANES), 1)
@@ -286,8 +286,8 @@
     lax.fori_loop(0, NZ, table_block, 0)
     scale = 4.0 / (peers * inner * NZ * NT)
     weight_ref[...] = scale / (kernel_mass + 4.0 * (modes_ref[...] + y_squares[col]))
-    last = relay(inner, 1, in_row, 0)
-    relay(outer, 0, in_column, last)
+    relay(inner // 2, col_before, col_after, 0)
+    relay(outer // 2, row_before, row_after, 2)
     top.wait()
 
     def prepare(i, carry):
@@ -563,7 +563,7 @@
             pltpu.SemaphoreType.DMA((8, 2)),
             pltpu.SemaphoreType.DMA((2, 3)),
             pltpu.SemaphoreType.DMA((2, 3)),
-            pltpu.SemaphoreType.REGULAR((2 * gx_count.bit_length(),)),
+            pltpu.SemaphoreType.REGULAR((4,)),
         ],
         compiler_params=pltpu.CompilerParams(collective_id=0, has_side_effects=True, **PARAMS),
         name="momentum_and_smooth",

time: 128 us -> 124 us (0.969)
  Pallas kernels: 127 us -> 123 us
    pallas_call x1, Pallas kernels: 124 us -> 120 us  [shards(): pl.pallas_call(functools.partial(step_kernel, inner, outer, hartley(inner...]
where the time goes in v3:
time: 124 us
  Pallas kernels  123 us (99%)
    pallas_call x1, Pallas kernels, shards(): pl.pallas_call(functools.partial(step_kernel, inner, outer, hartley(inner...  120 us
    pallas_call x1, Pallas kernels, shards(): pl.pallas_call(finish_kernel, grid=(sites // width,), out_shape=[jax.Shap...  3.49 us

profile of v3, /device:TPU:65, one launch (start us, length us, event | category | flops | bytes accessed | tf_op | source)
XLA Modules:
  0.0 123.8 jit_solution(4996116457484283220)
XLA Ops:
  0.6 119.6 %momentum_and_smooth.1 = (f32[8,8,1024]{2,1,0:T(8,128)}, f32[64,1024]{1,0:T(8,128)}) custom-call(f32[4,12,8,1024]{3,2,1,0:T(8,128)} %bitcast.8, f32[8,8,1024]{2,1,0:T(8,128)} %bitcast.10, f32[2,32,1024]{2,1,0:T(8,128)} %constant.10.clone.plane_hbm, f32[2,512,128]{2,1,0:T(8,128)} %constant.11.clone.modes_hbm, bf16[2,512,512]{2,1,0:T(8,128)(2,1)} %constant.20.x_hbm, ...), custom_call_target="tpu_custom_call" | custom-call | tf_op jit(solution)/shard_map/momentum_and_smooth/pallas_call | solution.py:530
  120.3 3.5 %link_update.1 = (f32[12,8,1024]{2,1,0:T(8,128)}, f32[8,8,1024]{2,1,0:T(8,128)}) custom-call(f32[64,1024]{1,0:T(8,128)} %get-tuple-element.6.smooth_ref, f32[4,12,8,1024]{3,2,1,0:T(8,128)} %bitcast.9, f32[8,8,1024]{2,1,0:T(8,128)} %get-tuple-element.7.momentum_ref), custom_call_target="tpu_custom_call" | custom-call | tf_op jit(solution)/shard_map/link_update/pallas_call | solution.py:573

commit v4 on v2

--- a/solution.py
+++ b/solution.py
@@ -176,7 +176,7 @@
     new_ref, smooth_ref,
     links_ref, ahead_ref, momentum_ref, plane_ref, modes_ref, x_ref,
     high_ref, low_ref, weight_ref, path_ref, partial_ref, staple_ref, behind_ref,
-    top_out, top_in, edge_out, edge_in,
+    turn_x, turn_t, parts_out, parts_in, top_out, top_in, edge_out, edge_in,
     plane_sum_ref, spectrum_ref, both_ref, bands_ref, whole_ref, done_ref, back_ref, halves_ref, filtered_ref,
     load_sems, halo_sems, swap_sems, all_sems, ring_sems,
 ):
@@ -235,10 +235,11 @@
     halos = [send(links_hbm.at[nu], ahead_ref.at[nu - 1], halo_sems.at[nu - 1], before) for nu in (1, 2)]
     quarters = 4
     width = sites // quarters
+    quarter = [pl.ds(q * width, width) for q in range(quarters)]
+    halos.append(send(links_hbm.at[0], turn_x, halo_sems.at[2], after))
     for q in range(quarters):
-        lanes = pl.ds(q * width, width)
         halos.append(
-            send(links_hbm.at[3, :, :, lanes], ahead_ref.at[2, :, :, lanes], halo_sems.at[2 + q], before)
+            send(links_hbm.at[3, :, :, quarter[q]], turn_t.at[:, :, quarter[q]], halo_sems.at[3 + q], after)
         )
     for halo in halos:
         halo.start()
@@ -269,7 +270,7 @@
         return carry
 
     lax.fori_loop(0, tiles, pack_top, 0)
-    top = send(top_out, top_in, halo_sems.at[2 + quarters], partner)
+    top = send(top_out, top_in, halo_sems.at[3 + quarters], partner)
     top.start()
 
     for load in loads[1:]:
@@ -287,7 +288,6 @@
     scale = 4.0 / (peers * inner * NZ * NT)
     weight_ref[...] = scale / (kernel_mass + 4.0 * (modes_ref[...] + y_squares[col]))
     last = relay(inner, 1, in_row, 0)
-    relay(outer, 0, in_column, last)
     top.wait()
 
     def prepare(i, carry):
@@ -305,13 +305,7 @@
                 pltpu.roll(links_ref[0, e, :, following], LANES - NT, 1),
             )
 
-        def moved_t(e):
-            value = links_ref[0, e, :, here]
-            return jnp.where(
-                t_site == NT - 1, pltpu.roll(value, NT - 1, 1), pltpu.roll(value, LANES - 1, 1)
-            )
-
-        for nu, moved in ((1, moved_y), (2, moved_z), (3, moved_t)):
+        for nu, moved in ((1, moved_y), (2, moved_z)):
             link_nu = matrix_of(lambda e: links_ref[nu, e, :, here])
             path = product(link_nu, matrix_of(moved))
             for r in range(3):
@@ -354,18 +348,45 @@
             behind_ref[e, :, here] = flat[e]
         return carry
 
+    def shift_t(value, forward):
+        if forward:
+            return jnp.where(
+                t_site == NT - 1, pltpu.roll(value, NT - 1, 1), pltpu.roll(value, LANES - 1, 1)
+            )
+        return jnp.where(t_site == 0, pltpu.roll(value, LANES - NT + 1, 1), pltpu.roll(value, 1, 1))
+
     def along_t(i, carry):
-        here, flat = staples(3, i)
-        for e in range(18):
-            staple_ref[e, :, here] += jnp.where(
-                t_site == 0, pltpu.roll(flat[e], LANES - NT + 1, 1), pltpu.roll(flat[e], 1, 1)
-            )
+        here = lanes_of(i)
+        link_x = matrix_of(lambda e: turn_x[e, :, here])
+        moved = matrix_of(lambda e: shift_t(turn_x[e, :, here], True))
+        link_t = matrix_of(lambda e: turn_t[e, :, here])
+        ahead = matrix_of(lambda e: links_ref[3, e, :, here])
+        corner = product(link_x, ahead)
+        lower = product(corner, link_t, adj_left=True)
+        lower = [[tuple(shift_t(v, False) for v in entry) for entry in line] for line in lower]
+        upper = algebra_parts(product(corner, product(link_t, moved), adj_right=True))
+        below = algebra_parts(product(link_x, lower))
+        for a in range(8):
+            parts_out[a, :, here] = upper[a] + below[a]
         return carry
 
     halos[0].wait_recv()
     lax.fori_loop(0, tiles, along_y, 0)
-    edge = send(edge_out, edge_in, halo_sems.at[3 + quarters], partner)
+    edge = send(edge_out, edge_in, halo_sems.at[4 + quarters], partner)
     edge.start()
+    relay(outer, 0, in_column, last)
+    per = tiles // quarters
+    returned = []
+    halos[2].wait_recv()
+    for q in range(quarters):
+        halos[3 + q].wait_recv()
+        lax.fori_loop(per * q, per * (q + 1), along_t, 0)
+        back = send(
+            parts_out.at[:, :, quarter[q]], parts_in.at[:, :, quarter[q]],
+            halo_sems.at[5 + quarters + q], before,
+        )
+        back.start()
+        returned.append(back)
     halos[1].wait_recv()
     lax.fori_loop(0, tiles, along_z, 0)
     edge.wait()
@@ -387,16 +408,14 @@
         link_x = matrix_of(lambda e: links_ref[0, e, :, here])
         parts = algebra_parts(product(link_x, staple))
         for a in range(8):
-            total = (coupling / 6.0) * (partial_ref[a, :, here] + parts[a])
+            total = (coupling / 6.0) * (partial_ref[a, :, here] + parts[a] + parts_in[a, :, here])
             new_ref[a, :, here] = momentum_ref[a, :, here] - step_force * total
         return carry
 
     count = new_ref.shape[0] * new_ref.shape[1]
     half = tiles // 2
-    per = tiles // quarters
     for q in range(quarters):
-        halos[2 + q].wait_recv()
-        lax.fori_loop(per * q, per * (q + 1), along_t, 0)
+        returned[q].wait_recv()
         lax.fori_loop(per * q, per * (q + 1), force, 0)
         taken = slice(q * width, (q + 1) * width)
         value = new_ref[:, :, taken].reshape(count, width)
@@ -496,7 +515,7 @@
     for pair in range(half):
         columns = slice(pair * 2 * LANES, (pair + 1) * 2 * LANES)
         smooth_ref[:, columns] = split_dot(value, high_ref, low_ref, columns)
-    for halo in halos:
+    for halo in halos + returned:
         halo.wait_send()
 
 
@@ -534,7 +553,7 @@
         out_specs=[VMEM] * 2,
         scratch_shapes=[
             pltpu.VMEM(links.shape, f32),
-            pltpu.VMEM((3,) + links.shape[1:], f32),
+            pltpu.VMEM((2,) + links.shape[1:], f32),
             pltpu.VMEM(field, f32),
             pltpu.VMEM(plane.shape, f32),
             pltpu.VMEM(modes.shape[1:], f32),
@@ -542,10 +561,14 @@
             pltpu.VMEM((sites, sites), bf16),
             pltpu.VMEM((sites, sites), bf16),
             pltpu.VMEM(modes.shape[1:], f32),
-            pltpu.VMEM((3,) + staple, f32),
+            pltpu.VMEM((2,) + staple, f32),
             pltpu.VMEM(field, f32),
             pltpu.VMEM(staple, f32),
             pltpu.VMEM(staple, f32),
+            pltpu.VMEM(links.shape[1:], f32),
+            pltpu.VMEM(links.shape[1:], f32),
+            pltpu.VMEM(field, f32),
+            pltpu.VMEM(field, f32),
             pltpu.VMEM((12, tiles, LANES), f32),
             pltpu.VMEM((12, tiles, LANES), f32),
             pltpu.VMEM((18, tiles, LANES), f32),
@@ -560,7 +583,7 @@
             pltpu.VMEM(halved, f32),
             pltpu.VMEM(halved, f32),
             pltpu.SemaphoreType.DMA((5,)),
-            pltpu.SemaphoreType.DMA((8, 2)),
+            pltpu.SemaphoreType.DMA((13, 2)),
             pltpu.SemaphoreType.DMA((2, 3)),
             pltpu.SemaphoreType.DMA((2, 3)),
             pltpu.SemaphoreType.REGULAR((2 * gx_count.bit_length(),)),

time: 128 us -> 120 us (0.938)
  Pallas kernels: 127 us -> 119 us
    pallas_call x1, Pallas kernels: 124 us -> 116 us  [shards(): pl.pallas_call(functools.partial(step_kernel, inner, outer, hartley(inner...]
where the time goes in v4:
time: 120 us
  Pallas kernels  119 us (99%)
    pallas_call x1, Pallas kernels, shards(): pl.pallas_call(functools.partial(step_kernel, inner, outer, hartley(inner...  116 us
    pallas_call x1, Pallas kernels, shards(): pl.pallas_call(finish_kernel, grid=(sites // width,), out_shape=[jax.Shap...  3.49 us

profile of v4, /device:TPU:65, one launch (start us, length us, event | category | flops | bytes accessed | tf_op | source)
XLA Modules:
  0.0 119.8 jit_solution(1564959147900967815)
XLA Ops:
  0.6 115.7 %momentum_and_smooth.1 = (f32[8,8,1024]{2,1,0:T(8,128)}, f32[64,1024]{1,0:T(8,128)}) custom-call(f32[4,12,8,1024]{3,2,1,0:T(8,128)} %bitcast.8, f32[8,8,1024]{2,1,0:T(8,128)} %bitcast.10, f32[2,32,1024]{2,1,0:T(8,128)} %constant.10.clone.plane_hbm, f32[2,512,128]{2,1,0:T(8,128)} %constant.11.clone.modes_hbm, bf16[2,512,512]{2,1,0:T(8,128)(2,1)} %constant.20.x_hbm, ...), custom_call_target="tpu_custom_call" | custom-call | tf_op jit(solution)/shard_map/momentum_and_smooth/pallas_call | solution.py:549
  116.3 3.5 %link_update.1 = (f32[12,8,1024]{2,1,0:T(8,128)}, f32[8,8,1024]{2,1,0:T(8,128)}) custom-call(f32[64,1024]{1,0:T(8,128)} %get-tuple-element.6.smooth_ref, f32[4,12,8,1024]{3,2,1,0:T(8,128)} %bitcast.9, f32[8,8,1024]{2,1,0:T(8,128)} %get-tuple-element.7.momentum_ref), custom_call_target="tpu_custom_call" | custom-call | tf_op jit(solution)/shard_map/link_update/pallas_call | solution.py:596

commit v5 on v4

--- a/solution.py
+++ b/solution.py
@@ -230,16 +230,17 @@
     for load in loads:
         load.start()
     pl.semaphore_wait(barrier, len(neighbours))
+    loads[0].wait()
 
     sites = new_ref.shape[2]
-    halos = [send(links_hbm.at[nu], ahead_ref.at[nu - 1], halo_sems.at[nu - 1], before) for nu in (1, 2)]
+    halos = [send(links_ref.at[nu], ahead_ref.at[nu - 1], halo_sems.at[nu - 1], before) for nu in (1, 2)]
     quarters = 4
     width = sites // quarters
     quarter = [pl.ds(q * width, width) for q in range(quarters)]
-    halos.append(send(links_hbm.at[0], turn_x, halo_sems.at[2], after))
+    halos.append(send(links_ref.at[0], turn_x, halo_sems.at[2], after))
     for q in range(quarters):
         halos.append(
-            send(links_hbm.at[3, :, :, quarter[q]], turn_t.at[:, :, quarter[q]], halo_sems.at[3 + q], after)
+            send(links_ref.at[3, :, :, quarter[q]], turn_t.at[:, :, quarter[q]], halo_sems.at[3 + q], after)
         )
     for halo in halos:
         halo.start()
@@ -262,7 +263,6 @@
     def lanes_of(i):
         return pl.ds(pl.multiple_of(i * LANES, LANES), LANES)
 
-    loads[0].wait()
 
     def pack_top(i, carry):
         for e in range(12):
@@ -485,12 +485,9 @@
     def transform(value):
         high = value.astype(bf16)
         low = (value - high.astype(f32)).astype(bf16)
-        table = x_ref[0]
-        return (
-            jnp.dot(table, high, preferred_element_type=f32)
-            + jnp.dot(table, low, preferred_element_type=f32)
-            + jnp.dot(x_ref[1], high, preferred_element_type=f32)
-        )
+        both = jnp.dot(x_ref[0], jnp.concatenate([high, low], axis=1), preferred_element_type=f32)
+        rest = jnp.dot(x_ref[1], high, preferred_element_type=f32)
+        return both[:, :LANES] + both[:, LANES:] + rest
 
     modes = transform(whole_ref[...].reshape(flat_shape)) * weight_ref[...]
     done_ref[...] = transform(modes).reshape(shape)

time: 120 us -> 119 us (level)
  no operation moved by 1% of the time
where the time goes in v5:
time: 119 us
  Pallas kernels  118 us (99%)
    pallas_call x1, Pallas kernels, shards(): pl.pallas_call(functools.partial(step_kernel, inner, outer, hartley(inner...  115 us
    pallas_call x1, Pallas kernels, shards(): pl.pallas_call(finish_kernel, grid=(sites // width,), out_shape=[jax.Shap...  3.49 us

profile of v5, /device:TPU:65, one launch (start us, length us, event | category | flops | bytes accessed | tf_op | source)
XLA Modules:
  0.0 118.9 jit_solution(3515277440045823172)
XLA Ops:
  0.6 114.8 %momentum_and_smooth.1 = (f32[8,8,1024]{2,1,0:T(8,128)}, f32[64,1024]{1,0:T(8,128)}) custom-call(f32[4,12,8,1024]{3,2,1,0:T(8,128)} %bitcast.8, f32[8,8,1024]{2,1,0:T(8,128)} %bitcast.10, f32[2,32,1024]{2,1,0:T(8,128)} %constant.10.clone.plane_hbm, f32[2,512,128]{2,1,0:T(8,128)} %constant.11.clone.modes_hbm, bf16[2,512,512]{2,1,0:T(8,128)(2,1)} %constant.20.x_hbm, ...), custom_call_target="tpu_custom_call" | custom-call | tf_op jit(solution)/shard_map/momentum_and_smooth/pallas_call | solution.py:546
  115.4 3.5 %link_update.1 = (f32[12,8,1024]{2,1,0:T(8,128)}, f32[8,8,1024]{2,1,0:T(8,128)}) custom-call(f32[64,1024]{1,0:T(8,128)} %get-tuple-element.6.smooth_ref, f32[4,12,8,1024]{3,2,1,0:T(8,128)} %bitcast.9, f32[8,8,1024]{2,1,0:T(8,128)} %get-tuple-element.7.momentum_ref), custom_call_target="tpu_custom_call" | custom-call | tf_op jit(solution)/shard_map/link_update/pallas_call | solution.py:593
